TPU v7x, 32 devices: a whole 2x2x4 slice. The times are simulated.
32 devices in a mesh: ga: 2 (over core), band: 16 (over z, y, x).
Axes of the slice: x: 2, y: 2, z: 4, core: 2. Of those that a mesh axis runs over, the one named last changes fastest.
Arguments:
- orbitals: bfloat16 [1024, 2, 16384], P('band', None, 'ga'), may hold values from -6 to 6
- projectors: bfloat16 [864, 2, 16384], P(None, None, ('ga', 'band')), may hold values from -0.03125 to 0.03125
- coupling: float32 [4, 18, 18], replicated, may hold values from -6 to 6
- species: int32 [48], replicated, may hold values from 0 to 3
- offsets: int32 [48], replicated, may hold values from 0 to 846, as said below
Outputs:
- applied: bfloat16 [1024, 2, 16384], P('band', None, 'ga')
Inputs may be any that keep to these rules, and one draw needn't show every extreme that they name: Each atom's 18 projectors are the 18 consecutive rows of projectors starting at its offset; offsets are multiples of 18, and the atoms' blocks are distinct and cover all 864 rows.
All inputs are finite; a program needn't handle non-finite values.
Results may differ from a plain program's by a relative error of at most 0.0049.
Values may be sent and summed in bfloat16 or wider, within the bound.
A program may use at most 64 MiB of HBM per device.

v0:
```python
import jax
import jax.numpy as jnp
from jax import lax
from jax.sharding import PartitionSpec as P


def block_matrices(coupling, species, offsets):
    per_atom = coupling.shape[1]
    count = offsets.shape[0]
    blocks = jnp.arange(count, dtype=jnp.int32)
    matches = (offsets[None, :] == blocks[:, None] * per_atom).astype(jnp.int32)
    atom_kind = jnp.sum(matches * species[None, :], axis=1)
    onehot = (atom_kind[:, None] == jnp.arange(coupling.shape[0], dtype=jnp.int32)[None, :]).astype(
        jnp.float32
    )
    table = coupling.reshape(coupling.shape[0], per_atom * per_atom)
    picked = jnp.dot(
        onehot, table, precision=lax.Precision.HIGHEST, preferred_element_type=jnp.float32
    )
    return picked.reshape(count, per_atom, per_atom)


def apply_coupling(matrices, becp):
    count = matrices.shape[0]
    per_atom = matrices.shape[1]
    height = becp.shape[0]
    widths = becp.shape[2]
    blocked = becp.reshape(count, per_atom, 2 * widths)
    coupled = jnp.einsum("aij,ajc->aic", matrices, blocked, precision=lax.Precision.HIGHEST)
    return coupled.reshape(height, 2, widths).astype(jnp.bfloat16)


def project_bands(projectors, spread):
    total_proj = projectors.shape[0]
    total_bands = spread.shape[0]
    flat_proj = projectors.reshape(total_proj, -1)
    turned = jnp.concatenate([spread[:, 1, :], -spread[:, 0, :]], axis=1)
    stacked = jnp.concatenate([spread.reshape(total_bands, -1), turned], axis=0)
    partial_value = lax.dot_general(
        flat_proj, stacked, (((1,), (1,)), ((), ())), preferred_element_type=jnp.float32
    )
    return partial_value.reshape(total_proj, 2, total_bands)


def add_back(projectors, dbecp):
    total_proj = projectors.shape[0]
    total_bands = dbecp.shape[2]
    columns = dbecp.reshape(total_proj, 2 * total_bands)
    real_part = lax.dot_general(
        columns, projectors[:, 0, :], (((0,), (0,)), ((), ())), preferred_element_type=jnp.float32
    )
    imag_part = lax.dot_general(
        columns, projectors[:, 1, :], (((0,), (0,)), ((), ())), preferred_element_type=jnp.float32
    )
    out_real = real_part[:total_bands] - imag_part[total_bands:]
    out_imag = imag_part[:total_bands] + real_part[total_bands:]
    return jnp.stack([out_real, out_imag], axis=1).astype(jnp.bfloat16)


def per_device(orbitals, projectors, coupling, species, offsets):
    matrices = block_matrices(coupling, species, offsets)
    spread = lax.all_to_all(orbitals, "band", split_axis=2, concat_axis=0, tiled=True)
    partial_value = project_bands(projectors, spread)
    becp = lax.psum(partial_value, ("ga", "band"))
    dbecp = apply_coupling(matrices, becp)
    result = add_back(projectors, dbecp)
    return lax.all_to_all(result, "band", split_axis=0, concat_axis=2, tiled=True)


def solution(mesh):
    placed = (P("band", None, "ga"), P(None, None, ("ga", "band")), P(), P(), P())
    return jax.shard_map(
        per_device, mesh=mesh, in_specs=placed, out_specs=P("band", None, "ga"), check_vma=False
    )
```

profile of v0, /device:TPU:0, one launch (start us, length us, event | category | flops | bytes accessed | tf_op | source)
XLA Modules:
  0.0 417.0 jit_solution(8911082358564989493)
XLA Ops:
  6.5 11.4 %copy.45 = bf16[64,2,8192]{0,1,2:T(2,128)(2,1)} copy(bf16[64,2,8192]{2,1,0:T(2,128)(2,1)} %param.5) | data formatting | bytes 4194304 | tf_op args[0]
  17.9 7.5 %reshape.39 = bf16[16,2,32768]{2,1,0:T(2,128)(2,1)} reshape(bf16[8192,2,64]{2,1,0:T(2,128)(2,1)} %bitcast.46) | data formatting | bytes 4194304
  25.4 0.0 copy-start
  25.4 8.5 %all-to-all-start = ((bf16[16,2,32768]{2,1,0:T(2,128)(2,1)}), bf16[16,2,32768]{2,1,0:T(2,128)(2,1)}, u32[]{:S(2)}, u32[]{:S(2)}) async-start(bf16[16,2,32768]{2,1,0:T(2,128)(2,1)} %reshape.39), calls=%async_computation | async-start | bytes 4194304 | tf_op jit(solution)/shard_map/all_to_all | solution.py:62
  34.0 0.0 all-reduce.2.cloned.1.call-start
  34.0 0.0 copy-done
  34.0 0.5 copy.60
  34.5 42.6 %all-to-all-done = bf16[16,2,32768]{2,1,0:T(2,128)(2,1)} async-done(((bf16[16,2,32768]{2,1,0:T(2,128)(2,1)}), bf16[16,2,32768]{2,1,0:T(2,128)(2,1)}, u32[]{:S(2)}, u32[]{:S(2)}) %all-to-all-start) | async-done | bytes 2097184 | tf_op jit(solution)/shard_map/all_to_all | solution.py:62
  77.1 7.4 %reshape.40 = bf16[8192,2,64]{2,1,0:T(2,128)(2,1)} reshape(bf16[16,2,32768]{2,1,0:T(2,128)(2,1)} %all-to-all-done) | data formatting | bytes 4194304
  84.4 10.6 %copy.55 = bf16[64,2,16,512]{3,0,2,1:T(8,128)(2,1)} copy(bf16[64,2,16,512]{0,1,3,2:T(2,128)(2,1)} %bitcast.44) | data formatting | bytes 4194304 | tf_op jit(solution)/shard_map/all_to_all | solution.py:62
  95.0 7.4 %copy.54 = bf16[64,2,16,512]{3,2,0,1:T(8,128)(2,1)} copy(bf16[64,2,16,512]{0,1,3,2:T(2,128)(2,1)} %bitcast.45) | data formatting | bytes 4194304 | tf_op jit(solution)/shard_map/all_to_all | solution.py:62
  102.4 0.0 copy-start.1
  102.4 1.8 slice_bitcast_fusion
  104.2 0.4 copy-done.1
  104.6 2.2 copy.47
  106.8 0.6 copy.59
  107.4 12.5 %fusion.6 = f32[864,2048]{1,0:T(8,128)} fusion(bf16[864,1024]{1,0:T(8,128)(2,1)S(1)} %bitcast.53, bf16[1024,512]{1,0:T(8,128)(2,1)S(1)} %get-tuple-element.8, bf16[1024,512]{1,0:T(8,128)(2,1)S(1)} %get-tuple-element.7, bf16[1024,1024]{1,0:T(8,128)(2,1)S(1)} %bitcast.52), kind=kOutput, calls=%fused_computation.6 | convolution fusion | flops 3636461568 | bytes 13041664 | tf_op jit(solution)/shard_map/dot_general | solution.py:39
  119.9 7.9 %reshape.36 = f32[48,18,2048]{2,1,0:T(8,128)} reshape(f32[864,2048]{1,0:T(8,128)} %fusion.6) | data formatting | bytes 14155776 | tf_op jit(solution)/shard_map/reshape | solution.py:28
  127.8 0.0 copy-start.5
  127.8 0.0 copy-start.6
  127.8 0.0 copy-start.7
  127.8 0.0 all-reduce.2.cloned.1.call-update
  127.8 0.7 copy-done.5
  128.6 0.1 reshape.32
  128.6 0.1 dot_general.22
  128.8 0.0 copy-done.6
  128.8 0.0 copy-done.7
  128.8 0.2 select_reduce_fusion
  128.9 0.4 fusion.16
  129.4 0.3 copy.49
  129.7 4.2 %fusion.22 = (bf16[864,1,512]{2,1,0:T(2,128)(2,1)}, bf16[864,1,512]{2,1,0:T(2,128)(2,1)}) fusion(bf16[864,2,512]{2,1,0:T(2,128)(2,1)S(1)} %copy-done), kind=kLoop, calls=%fused_computation.30 | loop fusion | bytes 3538944 | tf_op jit(solution)/shard_map/slice | solution.py:53
  133.9 189.5 %all-reduce.2.cloned.1.call-done = f32[48,18,2048]{2,1,0:T(8,128)} async-done(((f32[48,18,2048]{2,1,0:T(8,128)}), f32[48,18,2048]{2,1,0:T(8,128)}) %all-reduce.2.cloned.1.call-update) | async-done | bytes 7077904 | tf_op jit(solution)/shard_map/psum | solution.py:64
  323.4 12.2 %convolution_convert_fusion = bf16[48,18,2048]{2,1,0:T(8,128)(2,1)} fusion(f32[48,18,18]{2,1,0:T(8,128)S(1)} %copy.49, f32[48,18,2048]{2,1,0:T(8,128)} %all-reduce.2.cloned.1.call-done), kind=kOutput, calls=%fused_computation.7 | convolution fusion | flops 383975424 | bytes 10679040 | tf_op jit(solution)/shard_map/aij,ajc->aic/dot_general | solution.py:29
  335.5 0.0 copy-start.4
  335.5 6.2 %convert_element_type.12 = bf16[864,2048]{1,0:T(8,128)(2,1)} reshape(bf16[48,18,2048]{2,1,0:T(8,128)(2,1)} %convolution_convert_fusion) | data formatting | bytes 7077888 | tf_op jit(solution)/shard_map/convert_element_type | solution.py:30
  341.7 0.0 copy-done.4
  341.7 0.0 copy-start.2
  341.7 0.0 copy-start.3
  341.8 4.6 %fusion.14 = f32[2048,512]{1,0:T(8,128)S(1)} fusion(bf16[864,2048]{1,0:T(8,128)(2,1)} %convert_element_type.12, bf16[864,1,512]{2,1,0:T(2,128)(2,1)S(1)} %copy-done.4), kind=kOutput, calls=%fused_computation.19 | convolution fusion | flops 1811939328 | bytes 8617984 | tf_op jit(solution)/shard_map/dot_general | solution.py:52
  346.3 0.0 copy-done.2
  346.4 0.0 copy-done.3
  346.4 2.4 fusion.15
  348.8 1.2 fusion.11
  350.0 0.2 pad_maximum_fusion
  350.2 2.2 copy.52
  352.4 54.2 %all_to_all.36 = bf16[1024,2,512]{2,1,0:T(2,128)(2,1)S(1)} all-to-all(bf16[1024,2,512]{2,1,0:T(2,128)(2,1)S(1)} %copy.52), channel_id=1, replica_groups=mesh['ga'=2,'band'=16] {'band'}, dimensions={0} | all-to-all | bytes 4194304 | tf_op jit(solution)/shard_map/all_to_all | solution.py:67
  406.5 3.6 copy.58
  (2 shorter events, 0.0 us)
Async XLA Ops:
  25.4 8.6 %copy-start = (bf16[864,2,512]{2,1,0:T(2,128)(2,1)S(1)}, bf16[864,2,512]{2,1,0:T(2,128)(2,1)}, u32[]{:S(2)}) copy-start(bf16[864,2,512]{2,1,0:T(2,128)(2,1)} %param.6) | copy-start | bytes 5308420
  25.4 51.6 %all-to-all-start = ((bf16[16,2,32768]{2,1,0:T(2,128)(2,1)}), bf16[16,2,32768]{2,1,0:T(2,128)(2,1)}, u32[]{:S(2)}, u32[]{:S(2)}) async-start(bf16[16,2,32768]{2,1,0:T(2,128)(2,1)} %reshape.39), calls=%async_computation | async-start | bytes 4194304 | tf_op jit(solution)/shard_map/all_to_all | solution.py:62
  34.0 289.4 %all-reduce.2.cloned.1.call-start = ((), (), s32[]{:S(2)}) async-start(), calls=%async_computation.2 | async-start | bytes 18874368 | tf_op jit(solution)/shard_map/psum | solution.py:64
  102.4 2.2 copy-start.1
  127.8 0.8 copy-start.5
  127.8 1.0 copy-start.6
  127.8 1.0 copy-start.7
  335.5 6.2 %copy-start.4 = (bf16[864,1,512]{2,1,0:T(2,128)(2,1)S(1)}, bf16[864,1,512]{2,1,0:T(2,128)(2,1)}, u32[]{:S(2)}) copy-start(bf16[864,1,512]{2,1,0:T(2,128)(2,1)} %get-tuple-element.9) | copy-start | bytes 2654212
  341.7 4.6 %copy-start.2 = (bf16[864,2048]{1,0:T(8,128)(2,1)S(1)}, bf16[864,2048]{1,0:T(8,128)(2,1)}, u32[]{:S(2)}) copy-start(bf16[864,2048]{1,0:T(8,128)(2,1)} %convert_element_type.12) | copy-start | bytes 10616836
  341.7 4.6 %copy-start.3 = (bf16[864,1,512]{2,1,0:T(2,128)(2,1)S(1)}, bf16[864,1,512]{2,1,0:T(2,128)(2,1)}, u32[]{:S(2)}) copy-start(bf16[864,1,512]{2,1,0:T(2,128)(2,1)} %get-tuple-element.10) | copy-start | bytes 2654212
Sparse Core Ops, SparseCore 0:
  127.9 195.3 all-reduce.1
where the time goes:
time: 419 us; the launch traced here: 417 us
  waiting for transfers between devices  232 us (55%)
  local copies, waits for them, and re-layouts  73.2 us (17%)
  blocking collectives  54.2 us (13%)
  matrix products  32 us (8%)
  between operations  13.6 us (3%)
  starting transfers between devices  8.57 us (2%)
    psum x1, waiting for transfers between devices, per_device(): becp = lax.psum(partial_value, ('ga', 'band'))  189 us
    all_to_all x1, blocking collectives, per_device(): lax.all_to_all(result, 'band', split_axis=0, concat_axis=2, tiled=True)  54.2 us
    all_to_all x1, waiting for transfers between devices, per_device(): lax.all_to_all(orbitals, 'band', split_axis=2, concat_axis=0, tiled=True)  42.6 us
    unnamed x22, local copies, waits for them, and re-layouts  28.5 us
    all_to_all x3, local copies, waits for them, and re-layouts, per_device(): lax.all_to_all(orbitals, 'band', split_axis=2, concat_axis=0, tiled=True)  20.1 us
    dot_general x1, matrix products, project_bands(): lax.dot_general(flat_proj, stacked, (((1,), (1,)), ((), ())), preferred_e...  12.5 us
    dot_general x1, matrix products, apply_coupling(): jnp.einsum('aij,ajc->aic', matrices, blocked, precision=lax.Precision.HIG...  12.2 us
    all_to_all x1, starting transfers between devices, per_device(): lax.all_to_all(orbitals, 'band', split_axis=2, concat_axis=0, tiled=True)  8.52 us
  transfers between devices with their start and end apart: 2, of which 2 were waited for; matrix products, arithmetic and copies ran while one was open for 1% of the time, Pallas kernels for 0%

commit v1 on v0

--- a/solution.py
+++ b/solution.py
@@ -2,6 +2,17 @@
 import jax.numpy as jnp
 from jax import lax
 from jax.sharding import PartitionSpec as P
+
+
+def in_blocks(x, dim, size):
+    before, after = (x.shape[:dim], x.shape[dim + 1 :])
+    return jnp.moveaxis(x.reshape(*before, size, -1, *after), dim, 0)
+
+
+def laid_out(blocks, dim):
+    shape = list(blocks.shape[1:])
+    shape[dim] *= blocks.shape[0]
+    return jnp.moveaxis(blocks, 0, dim).reshape(shape)
 
 
 def block_matrices(coupling, species, offsets):
@@ -59,7 +70,14 @@
 
 def per_device(orbitals, projectors, coupling, species, offsets):
     matrices = block_matrices(coupling, species, offsets)
-    spread = lax.all_to_all(orbitals, "band", split_axis=2, concat_axis=0, tiled=True)
+    size, position = (lax.axis_size("band"), lax.axis_index("band"))
+    blocks_2 = in_blocks(orbitals, 2, size)
+    gathered = [blocks_2[position]]
+    for lap in range(1, size):
+        sent = blocks_2[position ^ lap]
+        gathered.append(lax.ppermute(sent, "band", [(i, i ^ lap) for i in range(size)]))
+    blocks_2 = jnp.stack(gathered)[position ^ jnp.arange(size)]
+    spread = laid_out(blocks_2, 0)
     partial_value = project_bands(projectors, spread)
     becp = lax.psum(partial_value, ("ga", "band"))
     dbecp = apply_coupling(matrices, becp)

time: 419 us -> 389 us (0.928)
  waiting for transfers between devices: 232 us -> 202 us
  starting transfers between devices: 8.57 us -> 33 us
  local copies, waits for them, and re-layouts: 73.2 us -> 52.5 us
    all_to_all x1 -> x0, waiting for transfers between devices: 42.6 us -> none  [per_device(): lax.all_to_all(orbitals, 'band', split_axis=2, concat_axis=0, tiled=True)]
    ppermute x0 -> x15, starting transfers between devices: none -> 33 us  [per_device(): lax.ppermute(sent, 'band', [(i, i ^ lap) for i in range(size)])]
    all_to_all x3 -> x0, local copies, waits for them, and re-layouts: 20.1 us -> none  [per_device(): lax.all_to_all(orbitals, 'band', split_axis=2, concat_axis=0, tiled=True)]
    ppermute x0 -> x15, waiting for transfers between devices: none -> 13.7 us  [per_device(): lax.ppermute(sent, 'band', [(i, i ^ lap) for i in range(size)])]
    unnamed x22 -> x47, local copies, waits for them, and re-layouts: 28.5 us -> 14.9 us
    all_to_all x1 -> x0, starting transfers between devices: 8.52 us -> none  [per_device(): lax.all_to_all(orbitals, 'band', split_axis=2, concat_axis=0, tiled=True)]
    another operation x0 -> x2, local copies, waits for them, and re-layouts: none -> 6.82 us
    gather x0 -> x3, local copies, waits for them, and re-layouts: none -> 4.66 us  [per_device(): blocks_2 = jnp.stack(gathered)[position ^ jnp.arange(size)]]
  transfers between devices with their start and end apart: 2 -> 16, of which waited for: 2 -> 4; matrix products, arithmetic and copies ran while one was open for 1% -> 5% of each run, Pallas kernels for 0% -> 0%
where the time goes in v1:
time: 389 us
  waiting for transfers between devices  202 us (52%)
  blocking collectives  54.2 us (14%)
  local copies, waits for them, and re-layouts  52.5 us (13%)
  starting transfers between devices  33 us (8%)
  matrix products  31.4 us (8%)
  between operations  13.8 us (4%)
    psum x1, waiting for transfers between devices, per_device(): becp = lax.psum(partial_value, ('ga', 'band'))  188 us
    all_to_all x1, blocking collectives, per_device(): lax.all_to_all(result, 'band', split_axis=0, concat_axis=2, tiled=True)  54.2 us
    ppermute x15, starting transfers between devices, per_device(): lax.ppermute(sent, 'band', [(i, i ^ lap) for i in range(size)])  33 us
    unnamed x47, local copies, waits for them, and re-layouts  14.9 us
    ppermute x15, waiting for transfers between devices, per_device(): lax.ppermute(sent, 'band', [(i, i ^ lap) for i in range(size)])  13.7 us
    dot_general x1, matrix products, project_bands(): lax.dot_general(flat_proj, stacked, (((1,), (1,)), ((), ())), preferred_e...  12.4 us
    dot_general x1, matrix products, apply_coupling(): jnp.einsum('aij,ajc->aic', matrices, blocked, precision=lax.Precision.HIG...  12.1 us
    reshape x1, local copies, waits for them, and re-layouts, apply_coupling(): blocked = becp.reshape(count, per_atom, 2 * widths)  7.9 us
  transfers between devices with their start and end apart: 16, of which 4 were waited for; matrix products, arithmetic and copies ran while one was open for 5% of the time, Pallas kernels for 0%

profile of v1, /device:TPU:0, one launch (start us, length us, event | category | flops | bytes accessed | tf_op | source)
XLA Modules:
  0.0 388.5 jit_solution(12306712407268415423)
XLA Ops:
  6.5 3.2 reshape.97
  9.9 6.2 %constant_dynamic-slice_fusion = (bf16[64,2,1,512]{3,2,1,0:T(2,128)(2,1)S(1)}, bf16[64,2,1,512]{3,2,1,0:T(2,128)(2,1)S(1)}, bf16[64,2,1,512]{3,2,1,0:T(2,128)(2,...) fusion(bf16[64,2,16,512]{3,2,1,0:T(8,128)(2,1)S(1)} %reshape.97, ...), kind=kLoop, calls=%fused_computation.59 | loop fusion | bytes 4194368 | tf_op jit(solution)/shard_map/dynamic-slice.15
  16.1 3.0 collective-permute-start
  19.1 1.6 collective-permute-start.1
  20.8 0.1 collective-permute-start.2
  20.9 2.1 collective-permute-start.3
  23.0 1.4 collective-permute-start.4
  24.5 0.7 fusion.16
  25.7 0.3 copy-done
  26.0 1.7 copy.126
  27.7 0.0 collective-permute-done
  27.7 2.6 collective-permute-start.5
  30.3 0.7 bitcast_dynamic-update-slice_fusion.14
  31.0 0.0 collective-permute-done.1
  31.0 0.7 bitcast_dynamic-update-slice_fusion.13
  31.7 3.0 collective-permute-start.7
  34.6 0.7 bitcast_dynamic-update-slice_fusion.12
  35.3 1.3 collective-permute-start.8
  36.6 0.7 bitcast_dynamic-update-slice_fusion.11
  37.2 3.5 collective-permute-start.9
  40.8 0.7 bitcast_dynamic-update-slice_fusion.10
  41.4 0.7 bitcast_dynamic-update-slice_fusion.9
  42.1 3.8 collective-permute-start.11
  46.0 0.7 bitcast_dynamic-update-slice_fusion.8
  46.6 7.1 %collective-permute-done.7 = bf16[64,2,512]{2,0,1:T(8,128)(2,1)S(1)} collective-permute-done((bf16[64,2,512]{2,0,1:T(8,128)(2,1)S(1)}, bf16[64,2,512]{2,0,1:T(8,128)(2,1)S(1)}, u32[]{:S(2)}, u32[]{:S(2)}) %collective-permute-start.7) | collective-permute-done | bytes 131104 | tf_op jit(solution)/shard_map/ppermute | solution.py:78
  53.7 3.9 %collective-permute-start.12 = (bf16[64,2,512]{2,0,1:T(8,128)(2,1)S(1)}, bf16[64,2,512]{2,0,1:T(8,128)(2,1)S(1)}, u32[]{:S(2)}, u32[]{:S(2)}) collective-permute-start(bf16[64,2,512]{2,0,1:T(8,128)(2,1)S(1)} %bitcast.143), channel_id=1, source_target_pairs={{0,13},{1,12},{2,15},{3,14},{4,9},{5,8},{6,11},{7,10},{8,5},{9,4},... | collective-permute-start | bytes 393224 | tf_op jit(solution)/shard_map/ppermute | solution.py:78
  57.6 0.7 bitcast_dynamic-update-slice_fusion.7
  58.3 2.9 collective-permute-start.13
  61.2 0.7 bitcast_dynamic-update-slice_fusion.6
  61.8 5.0 %collective-permute-done.9 = bf16[64,2,512]{2,0,1:T(8,128)(2,1)S(1)} collective-permute-done((bf16[64,2,512]{2,0,1:T(8,128)(2,1)S(1)}, bf16[64,2,512]{2,0,1:T(8,128)(2,1)S(1)}, u32[]{:S(2)}, u32[]{:S(2)}) %collective-permute-start.9) | collective-permute-done | bytes 131104 | tf_op jit(solution)/shard_map/ppermute | solution.py:78
  66.8 3.7 collective-permute-start.14
  70.6 0.7 bitcast_dynamic-update-slice_fusion.5
  71.2 0.7 bitcast_dynamic-update-slice_fusion.4
  71.9 0.7 bitcast_dynamic-update-slice_fusion.3
  72.6 0.7 bitcast_dynamic-update-slice_fusion.2
  73.2 0.7 bitcast_dynamic-update-slice_fusion.1
  73.9 1.6 collective-permute-done.14
  75.5 0.7 bitcast_dynamic-update-slice_fusion
  76.2 2.3 gather_fusion
  78.5 0.2 copy.35
  78.7 2.2 copy.34
  80.9 0.1 slice_bitcast_fusion
  81.0 0.6 copy.125
  81.6 0.9 copy-done.3
  82.5 12.4 %fusion.6 = f32[864,2048]{1,0:T(8,128)} fusion(bf16[864,1024]{1,0:T(8,128)(2,1)S(1)} %bitcast.140, bf16[1024,512]{1,0:T(8,128)(2,1)S(1)} %get-tuple-element.8, bf16[1024,512]{1,0:T(8,128)(2,1)S(1)} %get-tuple-element.7, bf16[1024,1024]{1,0:T(8,128)(2,1)S(1)} %bitcast.139), kind=kOutput, calls=%fused_computation.7 | convolution fusion | flops 3636461568 | bytes 13041664 | tf_op jit(solution)/shard_map/dot_general | solution.py:50
  94.8 7.9 %reshape.86 = f32[48,18,2048]{2,1,0:T(8,128)} reshape(f32[864,2048]{1,0:T(8,128)} %fusion.6) | data formatting | bytes 14155776 | tf_op jit(solution)/shard_map/reshape | solution.py:39
  102.8 0.0 all-reduce.2.cloned.1.call-update
  102.8 0.7 copy-done.4
  103.5 0.1 reshape.81
  103.6 0.1 dot_general.22
  103.7 0.2 select_reduce_fusion
  103.9 0.4 fusion.17
  104.3 0.3 copy.36
  104.6 4.2 %fusion.24 = (bf16[864,1,512]{2,1,0:T(2,128)(2,1)}, bf16[864,1,512]{2,1,0:T(2,128)(2,1)}) fusion(bf16[864,2,512]{2,1,0:T(2,128)(2,1)S(1)} %copy-done.1), kind=kLoop, calls=%fused_computation.82 | loop fusion | bytes 3538944 | tf_op jit(solution)/shard_map/slice | solution.py:64
  108.9 188.2 %all-reduce.2.cloned.1.call-done = f32[48,18,2048]{2,1,0:T(8,128)} async-done(((f32[48,18,2048]{2,1,0:T(8,128)}), f32[48,18,2048]{2,1,0:T(8,128)}) %all-reduce.2.cloned.1.call-update) | async-done | bytes 7077904 | tf_op jit(solution)/shard_map/psum | solution.py:82
  297.1 12.1 %convolution_convert_fusion = bf16[48,18,2048]{2,1,0:T(8,128)(2,1)} fusion(f32[48,18,18]{2,1,0:T(8,128)S(1)} %copy.36, f32[48,18,2048]{2,1,0:T(8,128)} %all-reduce.2.cloned.1.call-done), kind=kOutput, calls=%fused_computation.8 | convolution fusion | flops 383975424 | bytes 10679040 | tf_op jit(solution)/shard_map/aij,ajc->aic/dot_general | solution.py:40
  309.2 4.5 %convert_element_type.12 = bf16[864,2048]{1,0:T(8,128)(2,1)S(1)} reshape(bf16[48,18,2048]{2,1,0:T(8,128)(2,1)} %convolution_convert_fusion) | data formatting | bytes 7077888 | tf_op jit(solution)/shard_map/convert_element_type | solution.py:41
  313.8 4.0 %fusion.14 = f32[2048,512]{1,0:T(8,128)S(1)} fusion(bf16[864,2048]{1,0:T(8,128)(2,1)S(1)} %convert_element_type.12, bf16[864,1,512]{2,1,0:T(2,128)(2,1)} %get-tuple-element.25), kind=kOutput, calls=%fused_computation.20 | convolution fusion | flops 1811939328 | bytes 8617984 | tf_op jit(solution)/shard_map/dot_general | solution.py:63
  317.8 2.4 fusion.15
  320.2 1.2 fusion.11
  321.5 0.2 pad_maximum_fusion
  321.7 2.2 copy.39
  323.9 54.2 %all_to_all.18 = bf16[1024,2,512]{2,1,0:T(2,128)(2,1)S(1)} all-to-all(bf16[1024,2,512]{2,1,0:T(2,128)(2,1)S(1)} %copy.39), channel_id=1, replica_groups=mesh['ga'=2,'band'=16] {'band'}, dimensions={0} | all-to-all | bytes 4194304 | tf_op jit(solution)/shard_map/all_to_all | solution.py:85
  378.0 3.6 copy.124
  (43 shorter events, 0.7 us)
Async XLA Ops:
  6.5 290.5 %all-reduce.2.cloned.1.call-start = ((), (), s32[]{:S(2)}) async-start(), calls=%async_computation.1 | async-start | bytes 18874368 | tf_op jit(solution)/shard_map/psum | solution.py:82
  16.1 11.7 %collective-permute-start = (bf16[64,2,512]{2,0,1:T(8,128)(2,1)S(1)}, bf16[64,2,512]{2,0,1:T(8,128)(2,1)S(1)}, u32[]{:S(2)}, u32[]{:S(2)}) collective-permute-start(bf16[64,2,512]{2,0,1:T(8,128)(2,1)S(1)} %bitcast.155), channel_id=1, source_target_pairs={{0,1},{1,0},{2,3},{3,2},{4,5},{5,4},{6,7},{7,6},{8,9},{9,8},{10,11... | collective-permute-start | bytes 393224 | tf_op jit(solution)/shard_map/ppermute | solution.py:78
  19.1 11.9 %collective-permute-start.1 = (bf16[64,2,512]{2,0,1:T(8,128)(2,1)S(1)}, bf16[64,2,512]{2,0,1:T(8,128)(2,1)S(1)}, u32[]{:S(2)}, u32[]{:S(2)}) collective-permute-start(bf16[64,2,512]{2,0,1:T(8,128)(2,1)S(1)} %bitcast.154), channel_id=1, source_target_pairs={{0,2},{1,3},{2,0},{3,1},{4,6},{5,7},{6,4},{7,5},{8,10},{9,11},{10,... | collective-permute-start | bytes 393224 | tf_op jit(solution)/shard_map/ppermute | solution.py:78
  20.8 10.9 %collective-permute-start.2 = (bf16[64,2,512]{2,0,1:T(8,128)(2,1)S(1)}, bf16[64,2,512]{2,0,1:T(8,128)(2,1)S(1)}, u32[]{:S(2)}, u32[]{:S(2)}) collective-permute-start(bf16[64,2,512]{2,0,1:T(8,128)(2,1)S(1)} %bitcast.153), channel_id=1, source_target_pairs={{0,3},{1,2},{2,1},{3,0},{4,7},{5,6},{6,5},{7,4},{8,11},{9,10},{10,... | collective-permute-start | bytes 393224 | tf_op jit(solution)/shard_map/ppermute | solution.py:78
  20.9 14.4 %collective-permute-start.3 = (bf16[64,2,512]{2,0,1:T(8,128)(2,1)S(1)}, bf16[64,2,512]{2,0,1:T(8,128)(2,1)S(1)}, u32[]{:S(2)}, u32[]{:S(2)}) collective-permute-start(bf16[64,2,512]{2,0,1:T(8,128)(2,1)S(1)} %bitcast.152), channel_id=1, source_target_pairs={{0,4},{1,5},{2,6},{3,7},{4,0},{5,1},{6,2},{7,3},{8,12},{9,13},{10,... | collective-permute-start | bytes 393224 | tf_op jit(solution)/shard_map/ppermute | solution.py:78
  23.0 14.2 %collective-permute-start.4 = (bf16[64,2,512]{2,0,1:T(8,128)(2,1)S(1)}, bf16[64,2,512]{2,0,1:T(8,128)(2,1)S(1)}, u32[]{:S(2)}, u32[]{:S(2)}) collective-permute-start(bf16[64,2,512]{2,0,1:T(8,128)(2,1)S(1)} %bitcast.151), channel_id=1, source_target_pairs={{0,5},{1,4},{2,7},{3,6},{4,1},{5,0},{6,3},{7,2},{8,13},{9,12},{10,... | collective-permute-start | bytes 393224 | tf_op jit(solution)/shard_map/ppermute | solution.py:78
  24.5 1.5 copy-start
  27.7 13.7 %collective-permute-start.5 = (bf16[64,2,512]{2,0,1:T(8,128)(2,1)S(1)}, bf16[64,2,512]{2,0,1:T(8,128)(2,1)S(1)}, u32[]{:S(2)}, u32[]{:S(2)}) collective-permute-start(bf16[64,2,512]{2,0,1:T(8,128)(2,1)S(1)} %bitcast.150), channel_id=1, source_target_pairs={{0,6},{1,7},{2,4},{3,5},{4,2},{5,3},{6,0},{7,1},{8,14},{9,15},{10,... | collective-permute-start | bytes 393224 | tf_op jit(solution)/shard_map/ppermute | solution.py:78
  31.0 11.1 %collective-permute-start.6 = (bf16[64,2,512]{2,0,1:T(8,128)(2,1)S(1)}, bf16[64,2,512]{2,0,1:T(8,128)(2,1)S(1)}, u32[]{:S(2)}, u32[]{:S(2)}) collective-permute-start(bf16[64,2,512]{2,0,1:T(8,128)(2,1)S(1)} %bitcast.149), channel_id=1, source_target_pairs={{0,7},{1,6},{2,5},{3,4},{4,3},{5,2},{6,1},{7,0},{8,15},{9,14},{10,... | collective-permute-start | bytes 393224 | tf_op jit(solution)/shard_map/ppermute | solution.py:78
  31.7 22.0 %collective-permute-start.7 = (bf16[64,2,512]{2,0,1:T(8,128)(2,1)S(1)}, bf16[64,2,512]{2,0,1:T(8,128)(2,1)S(1)}, u32[]{:S(2)}, u32[]{:S(2)}) collective-permute-start(bf16[64,2,512]{2,0,1:T(8,128)(2,1)S(1)} %bitcast.148), channel_id=1, source_target_pairs={{0,8},{1,9},{2,10},{3,11},{4,12},{5,13},{6,14},{7,15},{8,0},{9,1},... | collective-permute-start | bytes 393224 | tf_op jit(solution)/shard_map/ppermute | solution.py:78
  35.3 23.0 %collective-permute-start.8 = (bf16[64,2,512]{2,0,1:T(8,128)(2,1)S(1)}, bf16[64,2,512]{2,0,1:T(8,128)(2,1)S(1)}, u32[]{:S(2)}, u32[]{:S(2)}) collective-permute-start(bf16[64,2,512]{2,0,1:T(8,128)(2,1)S(1)} %bitcast.147), channel_id=1, source_target_pairs={{0,9},{1,8},{2,11},{3,10},{4,13},{5,12},{6,15},{7,14},{8,1},{9,0},... | collective-permute-start | bytes 393224 | tf_op jit(solution)/shard_map/ppermute | solution.py:78
  37.2 29.6 %collective-permute-start.9 = (bf16[64,2,512]{2,0,1:T(8,128)(2,1)S(1)}, bf16[64,2,512]{2,0,1:T(8,128)(2,1)S(1)}, u32[]{:S(2)}, u32[]{:S(2)}) collective-permute-start(bf16[64,2,512]{2,0,1:T(8,128)(2,1)S(1)} %bitcast.146), channel_id=1, source_target_pairs={{0,10},{1,11},{2,8},{3,9},{4,14},{5,15},{6,12},{7,13},{8,2},{9,3},... | collective-permute-start | bytes 393224 | tf_op jit(solution)/shard_map/ppermute | solution.py:78
  41.4 29.8 %collective-permute-start.10 = (bf16[64,2,512]{2,0,1:T(8,128)(2,1)S(1)}, bf16[64,2,512]{2,0,1:T(8,128)(2,1)S(1)}, u32[]{:S(2)}, u32[]{:S(2)}) collective-permute-start(bf16[64,2,512]{2,0,1:T(8,128)(2,1)S(1)} %bitcast.145), channel_id=1, source_target_pairs={{0,11},{1,10},{2,9},{3,8},{4,15},{5,14},{6,13},{7,12},{8,3},{9,2},... | collective-permute-start | bytes 393224 | tf_op jit(solution)/shard_map/ppermute | solution.py:78
  42.1 29.8 %collective-permute-start.11 = (bf16[64,2,512]{2,0,1:T(8,128)(2,1)S(1)}, bf16[64,2,512]{2,0,1:T(8,128)(2,1)S(1)}, u32[]{:S(2)}, u32[]{:S(2)}) collective-permute-start(bf16[64,2,512]{2,0,1:T(8,128)(2,1)S(1)} %bitcast.144), channel_id=1, source_target_pairs={{0,12},{1,13},{2,14},{3,15},{4,8},{5,9},{6,10},{7,11},{8,4},{9,5},... | collective-permute-start | bytes 393224 | tf_op jit(solution)/shard_map/ppermute | solution.py:78
  53.7 18.9 %collective-permute-start.12 = (bf16[64,2,512]{2,0,1:T(8,128)(2,1)S(1)}, bf16[64,2,512]{2,0,1:T(8,128)(2,1)S(1)}, u32[]{:S(2)}, u32[]{:S(2)}) collective-permute-start(bf16[64,2,512]{2,0,1:T(8,128)(2,1)S(1)} %bitcast.143), channel_id=1, source_target_pairs={{0,13},{1,12},{2,15},{3,14},{4,9},{5,8},{6,11},{7,10},{8,5},{9,4},... | collective-permute-start | bytes 393224 | tf_op jit(solution)/shard_map/ppermute | solution.py:78
  58.3 14.9 %collective-permute-start.13 = (bf16[64,2,512]{2,0,1:T(8,128)(2,1)S(1)}, bf16[64,2,512]{2,0,1:T(8,128)(2,1)S(1)}, u32[]{:S(2)}, u32[]{:S(2)}) collective-permute-start(bf16[64,2,512]{2,0,1:T(8,128)(2,1)S(1)} %bitcast.142), channel_id=1, source_target_pairs={{0,14},{1,15},{2,12},{3,13},{4,10},{5,11},{6,8},{7,9},{8,6},{9,7},... | collective-permute-start | bytes 393224 | tf_op jit(solution)/shard_map/ppermute | solution.py:78
  66.8 8.7 %collective-permute-start.14 = (bf16[64,2,512]{2,0,1:T(8,128)(2,1)S(1)}, bf16[64,2,512]{2,0,1:T(8,128)(2,1)S(1)}, u32[]{:S(2)}, u32[]{:S(2)}) collective-permute-start(bf16[64,2,512]{2,0,1:T(8,128)(2,1)S(1)} %bitcast.141), channel_id=1, source_target_pairs={{0,15},{1,14},{2,13},{3,12},{4,11},{5,10},{6,9},{7,8},{8,7},{9,6},... | collective-permute-start | bytes 393224 | tf_op jit(solution)/shard_map/ppermute | solution.py:78
  81.0 1.5 copy-start.3
  102.7 0.8 copy-start.4
  102.7 1.0 copy-start.5
  102.8 1.0 copy-start.6
  102.8 1.9 copy-start.1
  313.7 4.1 %copy-start.2 = (bf16[864,1,512]{2,1,0:T(2,128)(2,1)S(1)}, bf16[864,1,512]{2,1,0:T(2,128)(2,1)}, u32[]{:S(2)}) copy-start(bf16[864,1,512]{2,1,0:T(2,128)(2,1)} %get-tuple-element.26) | copy-start | bytes 2654212
Sparse Core Ops, SparseCore 0:
  102.9 194.1 all-reduce.1
